TPU v7x, 32 devices: a whole 2x2x4 slice. The times are simulated.
32 devices in a mesh: grp: 4 (over z), hap: 8 (over y, x, core).
Axes of the slice: x: 2, y: 2, z: 4, core: 2. Of those that a mesh axis runs over, the one named last changes fastest.
Arguments:
- alleles: int32 [60, 512], P('grp', 'hap'), may hold values from 0 to 1073741823
- observed: int32 [60, 32], P('grp', 'hap'), may hold values from 0 to 2
- map_steps: int32 [60], P('grp'), may hold values from 1 to 99
- start_weights: float32 [32, 15360], P('hap'), may hold values from 1e-12 to 1
- end_weights: float32 [32, 15360], P('hap'), may hold values from 1e-12 to 1
Outputs:
- dosage: float32 [60, 32], P('grp', 'hap')
Inputs may be any that keep to these rules, and one draw needn't show every extreme that they name: Bit b of alleles[m, w] is the allele 0 or 1 of reference haplotype 30 w + b at marker m. 0 and 1 are observed alleles, 2 marks a marker not typed in that target.
All inputs are finite; a program needn't handle non-finite values.
Results may differ from a plain program's by a relative error of at most 0.0008.
Values sent between devices are 32-bit elements; how exact they have to be, the bound alone decides.
A program may use at most 128 MiB of HBM per device.

v0:
```python
import jax
import jax.numpy as jnp
from jax import lax
from jax.sharding import PartitionSpec as P

error_rate = 0.01
map_unit = 100000.0


def passed_along(value, axis, steps):
    count = lax.axis_size(axis)
    initial, last = (max(0, -steps), min(count, count - steps))
    return lax.ppermute(value, axis, [(source, source + steps) for source in range(initial, last)])


def unpack_alleles(packed):
    shifts = jnp.arange(30, dtype=jnp.int32)
    bits = jnp.bitwise_and(jnp.right_shift(packed[:, :, None], shifts[None, None, :]), 1)
    return bits.reshape(packed.shape[0], packed.shape[1] * 30).astype(jnp.float32)


def emission(allele_row, observed_col):
    missing = (observed_col == 2).astype(jnp.float32)[:, None]
    called = observed_col.astype(jnp.float32)[:, None]
    agree = allele_row[None, :] * called + (1.0 - allele_row[None, :]) * (1.0 - called)
    return missing + (1.0 - missing) * (error_rate + (1.0 - 2.0 * error_rate) * agree)


def forward_pass(state, haplos, observed, rates):
    total_haps = haplos.shape[1]

    def advance(carry, inputs):
        allele_row, observed_col, rate = inputs
        mixed = (1.0 - rate) * carry + rate / total_haps * jnp.sum(carry, axis=1, keepdims=True)
        weighted = emission(allele_row, observed_col) * mixed
        weighted = weighted / jnp.sum(weighted, axis=1, keepdims=True)
        return (weighted, weighted.astype(jnp.bfloat16))

    return lax.scan(advance, state, (haplos, observed, rates))


def backward_pass(state, haplos, observed, rates):
    total_haps = haplos.shape[1]

    def retreat(carry, inputs):
        allele_row, observed_col, rate = inputs
        kept = carry.astype(jnp.bfloat16)
        weighted = emission(allele_row, observed_col) * carry
        mixed = (1.0 - rate) * weighted + rate / total_haps * jnp.sum(
            weighted, axis=1, keepdims=True
        )
        mixed = mixed / jnp.sum(mixed, axis=1, keepdims=True)
        return (mixed, kept)

    return lax.scan(retreat, state, (haplos, observed, rates), reverse=True)


def keep_state(operands):
    return operands


def finish_dosage(forward_store, backward_store, haplos):
    allele_half = haplos.astype(jnp.bfloat16)
    carrying = backward_store * allele_half[:, None, :]
    numer = jnp.einsum("mtk,mtk->mt", forward_store, carrying, preferred_element_type=jnp.float32)
    denom = jnp.einsum(
        "mtk,mtk->mt", forward_store, backward_store, preferred_element_type=jnp.float32
    )
    return numer / denom


def local(alleles, observed, map_steps, start_weights, end_weights):
    packed = lax.all_gather(alleles, "hap", axis=1, tiled=True)
    start_rows = start_weights / jnp.sum(start_weights, axis=1, keepdims=True)
    end_rows = end_weights / jnp.sum(end_weights, axis=1, keepdims=True)
    position = lax.axis_index("grp")
    groups = lax.axis_size("grp")
    is_first = position == 0
    is_last = position == groups - 1
    targets = observed.shape[1]
    local_markers = observed.shape[0]
    haplos = unpack_alleles(packed)
    rates = 1.0 - jnp.exp(-map_steps.astype(jnp.float32) / map_unit)
    store_shape = (local_markers, targets, haplos.shape[1])
    forward_store = jnp.zeros(store_shape, jnp.bfloat16)
    backward_store = jnp.zeros(store_shape, jnp.bfloat16)

    def run_forward(operands):
        incoming, kept = operands
        begin = jnp.where(is_first, start_rows, incoming)
        return forward_pass(begin, haplos, observed, rates)

    def run_backward(operands):
        incoming, kept = operands
        begin = jnp.where(is_last, end_rows, incoming)
        return backward_pass(begin, haplos, observed, rates)

    def sweep_turn(section, carry):
        forward_in, backward_in, forward_kept, backward_kept = carry
        forward_out, forward_kept = lax.cond(
            section == position, run_forward, keep_state, (forward_in, forward_kept)
        )
        backward_out, backward_kept = lax.cond(
            section == groups - 1 - position, run_backward, keep_state, (backward_in, backward_kept)
        )
        forward_next = passed_along(forward_out, "grp", 1)
        backward_next = passed_along(backward_out, "grp", -1)
        return (forward_next, backward_next, forward_kept, backward_kept)

    result = lax.fori_loop(
        0, groups, sweep_turn, (start_rows, end_rows, forward_store, backward_store)
    )
    return finish_dosage(result[2], result[3], haplos)


def solution(mesh):
    in_specs = (P("grp", "hap"), P("grp", "hap"), P("grp"), P("hap", None), P("hap", None))
    out_specs = P("grp", "hap")
    return jax.shard_map(local, mesh=mesh, in_specs=in_specs, out_specs=out_specs, check_vma=False)
```

profile of v0, /device:TPU:0, one launch (start us, length us, event | category | flops | bytes accessed | tf_op | source)
XLA Modules:
  0.0 377.4 jit_solution(11413516875527414664)
XLA Ops:
  3.9 10.7 %all-gather = s32[8,64,15]{1,2,0:T(8,128)S(1)} all-gather(s32[1,64,15]{1,2,0:T(8,128)S(1)} %bitcast.55), channel_id=1, replica_groups=mesh['grp'=4,'hap'=8] {'hap'}, dimensions={0}, use_global_device_ids=true | all-gather | bytes 34560 | tf_op jit(solution)/shard_map/all_gather | solution.py:73
  14.8 1.7 broadcast.155
  16.6 1.7 broadcast.155.clone
  18.3 346.0 %while.49 = (s32[]{:T(128)}, f32[4,15360]{1,0:T(4,128)S(1)}, f32[4,15360]{1,0:T(4,128)S(1)}, bf16[15,4,15360]{2,1,0:T(4,128)(2,1)}, bf16[15,4,15360]{2,1,0:T(4,1...) while((s32[]{:T(128)}, f32[4,15360]{1,0:T(4,128)S(1)}, ...), condition=%wide.region_15.16_spmd.clone, body=%wide.region_2.15_spmd.clone.sunk | while | flops 2688047 | bytes 15024031 | solution.py:110
  18.3 3.5 shift_right_arithmetic.56
  21.8 3.9 %shift_right_arithmetic.57 = s32[15,15360]{1,0:T(8,128)S(1)} reshape(s32[15,512,30]{2,1,0:T(8,128)} %shift_right_arithmetic.56) | data formatting | bytes 1843200 | tf_op jit(solution)/shard_map/shift_right_arithmetic | solution.py:18
  25.8 51.5 %conditional.6 = ((f32[4,15360]{1,0:T(4,128)S(1)}, bf16[15,4,15360]{2,1,0:T(4,128)(2,1)})) conditional(s32[]{:T(128)} %convert_element_type.150, (f32[4,15360]{1,0:T(4,128)S(1)}, bf16[15,4,15360]{2,1,0:T(4,128)(2,1)}) %tuple.122, (pred[]{:T(512)}, f32[4,15360]{1,0:T(4,128)S(1)}, f32[4,15360]{1,0:T(4,128)S(1)}, s32[15,4]{1,0:T(8,128)S(1)}, ...), branch_computations={%region_3.0_spmd, %region_4.8_spmd} | conditional | flops 936980 | bytes 2397182 | solution.py:100
  25.9 51.4 %while.47 = (s32[]{:T(128)}, f32[4,15360]{1,0:T(4,128)S(1)}, bf16[15,4,15360]{2,1,0:T(4,128)(2,1)}, s32[15,4]{1,0:T(8,128)S(1)}, f32[15,15360]{1,0:T(8,128)S(1)}...) while((s32[]{:T(128)}, f32[4,15360]{1,0:T(4,128)S(1)}, ...), condition=%wide.region_8.7_spmd, body=%wide.region_5.6_spmd.sunk | while | flops 875540 | bytes 1659789 | solution.py:39
  77.3 1.3 collective-permute-start
  78.6 1.3 collective-permute-start.1
  79.9 4.6 %collective-permute-done = f32[4,15360]{1,0:T(4,128)S(1)} collective-permute-done((f32[4,15360]{1,0:T(4,128)S(1)}, f32[4,15360]{1,0:T(4,128)S(1)}, u32[]{:S(2)}, u32[]{:S(2)}) %collective-permute-start) | collective-permute-done | bytes 245792 | tf_op jit(solution)/shard_map/while/body/eval_jaxpr/ppermute | solution.py:13
  84.6 4.1 %collective-permute-done.1 = f32[4,15360]{1,0:T(4,128)S(1)} collective-permute-done((f32[4,15360]{1,0:T(4,128)S(1)}, f32[4,15360]{1,0:T(4,128)S(1)}, u32[]{:S(2)}, u32[]{:S(2)}) %collective-permute-start.1) | collective-permute-done | bytes 245792 | tf_op jit(solution)/shard_map/while/body/eval_jaxpr/ppermute | solution.py:13
  88.8 3.5 shift_right_arithmetic.56
  92.3 3.9 %shift_right_arithmetic.57 = s32[15,15360]{1,0:T(8,128)S(1)} reshape(s32[15,512,30]{2,1,0:T(8,128)} %shift_right_arithmetic.56) | data formatting | bytes 1843200 | tf_op jit(solution)/shard_map/shift_right_arithmetic | solution.py:18
  96.3 52.9 %collective-permute-start = (f32[4,15360]{1,0:T(4,128)S(1)}, f32[4,15360]{1,0:T(4,128)S(1)}, u32[]{:S(2)}, u32[]{:S(2)}) collective-permute-start(f32[4,15360]{1,0:T(4,128)S(1)} %get-tuple-element.844), channel_id=1, source_target_pairs={{0,8},{8,16},{16,24},{1,9},{9,17},{17,25},{2,10},{10,18},{18,26},{... | collective-permute-start | bytes 737288 | tf_op jit(solution)/shard_map/while/body/eval_jaxpr/ppermute | solution.py:13
  150.5 3.5 collective-permute-done
  154.1 4.1 %collective-permute-done.1 = f32[4,15360]{1,0:T(4,128)S(1)} collective-permute-done((f32[4,15360]{1,0:T(4,128)S(1)}, f32[4,15360]{1,0:T(4,128)S(1)}, u32[]{:S(2)}, u32[]{:S(2)}) %collective-permute-start.1) | collective-permute-done | bytes 245792 | tf_op jit(solution)/shard_map/while/body/eval_jaxpr/ppermute | solution.py:13
  158.2 3.5 shift_right_arithmetic.56
  161.7 3.9 %shift_right_arithmetic.57 = s32[15,15360]{1,0:T(8,128)S(1)} reshape(s32[15,512,30]{2,1,0:T(8,128)} %shift_right_arithmetic.56) | data formatting | bytes 1843200 | tf_op jit(solution)/shard_map/shift_right_arithmetic | solution.py:18
  165.8 10.0 %collective-permute-start = (f32[4,15360]{1,0:T(4,128)S(1)}, f32[4,15360]{1,0:T(4,128)S(1)}, u32[]{:S(2)}, u32[]{:S(2)}) collective-permute-start(f32[4,15360]{1,0:T(4,128)S(1)} %get-tuple-element.844), channel_id=1, source_target_pairs={{0,8},{8,16},{16,24},{1,9},{9,17},{17,25},{2,10},{10,18},{18,26},{... | collective-permute-start | bytes 737288 | tf_op jit(solution)/shard_map/while/body/eval_jaxpr/ppermute | solution.py:13
  177.1 3.2 collective-permute-done
  180.3 110.0 %collective-permute-done.1 = f32[4,15360]{1,0:T(4,128)S(1)} collective-permute-done((f32[4,15360]{1,0:T(4,128)S(1)}, f32[4,15360]{1,0:T(4,128)S(1)}, u32[]{:S(2)}, u32[]{:S(2)}) %collective-permute-start.1) | collective-permute-done | bytes 245792 | tf_op jit(solution)/shard_map/while/body/eval_jaxpr/ppermute | solution.py:13
  290.3 3.5 shift_right_arithmetic.56
  293.8 3.9 %shift_right_arithmetic.57 = s32[15,15360]{1,0:T(8,128)S(1)} reshape(s32[15,512,30]{2,1,0:T(8,128)} %shift_right_arithmetic.56) | data formatting | bytes 1843200 | tf_op jit(solution)/shard_map/shift_right_arithmetic | solution.py:18
  297.8 3.7 collective-permute-start
  301.5 54.7 %conditional.7 = ((f32[4,15360]{1,0:T(4,128)S(1)}, bf16[15,4,15360]{2,1,0:T(4,128)(2,1)})) conditional(s32[]{:T(128)} %convert_element_type.151, (f32[4,15360]{1,0:T(4,128)S(1)}, bf16[15,4,15360]{2,1,0:T(4,128)(2,1)}) %tuple.124, (pred[]{:T(512)}, f32[4,15360]{1,0:T(4,128)S(1)}, f32[4,15360]{1,0:T(4,128)S(1)}, f32[15]{0:T(128)S(1)}, ...), branch_computations={%region_9.9_spmd, %region_10.14_spmd} | conditional | flops 1059861 | bytes 4977184 | solution.py:103
  301.6 1.7 broadcast.151
  303.3 52.8 %while.48 = (s32[]{:T(128)}, f32[4,15360]{1,0:T(4,128)S(1)}, bf16[15,4,15360]{2,1,0:T(4,128)(2,1)}, f32[15]{0:T(128)S(1)}, s32[15,4]{1,0:T(8,128)S(1)}, /*index=...) while((s32[]{:T(128)}, f32[4,15360]{1,0:T(4,128)S(1)}, ...), condition=%wide.region_14.13_spmd, body=%wide.region_11.12_spmd.sunk | while | flops 998421 | bytes 2396589 | solution.py:55
  357.5 6.8 %collective-permute-done.1 = f32[4,15360]{1,0:T(4,128)S(1)} collective-permute-done((f32[4,15360]{1,0:T(4,128)S(1)}, f32[4,15360]{1,0:T(4,128)S(1)}, u32[]{:S(2)}, u32[]{:S(2)}) %collective-permute-start.1) | collective-permute-done | bytes 245792 | tf_op jit(solution)/shard_map/while/body/eval_jaxpr/ppermute | solution.py:13
  364.3 3.5 shift_right_arithmetic.24
  367.8 4.0 %shift_right_arithmetic.25 = s32[15,15360]{1,0:T(8,128)S(1)} reshape(s32[15,512,30]{2,1,0:T(8,128)} %shift_right_arithmetic.24) | data formatting | bytes 1843200 | tf_op jit(solution)/shard_map/shift_right_arithmetic | solution.py:18
  372.0 4.7 %fusion.7 = (f32[15,4]{1,0:T(8,128)S(1)}, f32[15,4]{1,0:T(8,128)S(1)}) fusion(bf16[15,4,15360]{2,1,0:T(4,128)(2,1)S(1)} %copy-done, bf16[15,4,15360]{2,1,0:T(4,128)(2,1)} %get-tuple-element.488, bf16[15,15360]{1,0:T(8,128)(2,1)S(1)} %convert_convert_fusion), kind=kLoop, calls=%fused_computation.33 | loop fusion | flops 7372680 | bytes 4147680
  (273 shorter events, 74.7 us)
Async XLA Ops:
  0.0 3.9 %copy-start.1 = (s32[15,64]{1,0:T(8,128)S(1)}, s32[15,64]{1,0:T(8,128)}, u32[]{:S(2)}) copy-start(s32[15,64]{1,0:T(8,128)} %param.15) | copy-start | bytes 11524
  0.0 14.7 %copy-start.2 = (s32[15,4]{0,1:T(4,128)S(1)}, s32[15,4]{0,1:T(4,128)}, u32[]{:S(2)}) copy-start(s32[15,4]{0,1:T(4,128)} %param.16) | copy-start | bytes 724
  0.0 14.8 %copy-start.3 = (s32[15]{0:T(128)S(1)}, s32[15]{0:T(128)}, u32[]{:S(2)}) copy-start(s32[15]{0:T(128)} %param.17) | copy-start | bytes 184
  77.3 7.3 %collective-permute-start = (f32[4,15360]{1,0:T(4,128)S(1)}, f32[4,15360]{1,0:T(4,128)S(1)}, u32[]{:S(2)}, u32[]{:S(2)}) collective-permute-start(f32[4,15360]{1,0:T(4,128)S(1)} %get-tuple-element.844), channel_id=1, source_target_pairs={{0,8},{8,16},{16,24},{1,9},{9,17},{17,25},{2,10},{10,18},{18,26},{... | collective-permute-start | bytes 737288 | tf_op jit(solution)/shard_map/while/body/eval_jaxpr/ppermute | solution.py:13
  78.6 10.1 %collective-permute-start.1 = (f32[4,15360]{1,0:T(4,128)S(1)}, f32[4,15360]{1,0:T(4,128)S(1)}, u32[]{:S(2)}, u32[]{:S(2)}) collective-permute-start(f32[4,15360]{1,0:T(4,128)S(1)} %get-tuple-element.845), channel_id=1, source_target_pairs={{8,0},{16,8},{24,16},{9,1},{17,9},{25,17},{10,2},{18,10},{26,18},{... | collective-permute-start | bytes 737288 | tf_op jit(solution)/shard_map/while/body/eval_jaxpr/ppermute | solution.py:13
  96.3 57.8 %collective-permute-start = (f32[4,15360]{1,0:T(4,128)S(1)}, f32[4,15360]{1,0:T(4,128)S(1)}, u32[]{:S(2)}, u32[]{:S(2)}) collective-permute-start(f32[4,15360]{1,0:T(4,128)S(1)} %get-tuple-element.844), channel_id=1, source_target_pairs={{0,8},{8,16},{16,24},{1,9},{9,17},{17,25},{2,10},{10,18},{18,26},{... | collective-permute-start | bytes 737288 | tf_op jit(solution)/shard_map/while/body/eval_jaxpr/ppermute | solution.py:13
  149.2 9.0 %collective-permute-start.1 = (f32[4,15360]{1,0:T(4,128)S(1)}, f32[4,15360]{1,0:T(4,128)S(1)}, u32[]{:S(2)}, u32[]{:S(2)}) collective-permute-start(f32[4,15360]{1,0:T(4,128)S(1)} %get-tuple-element.845), channel_id=1, source_target_pairs={{8,0},{16,8},{24,16},{9,1},{17,9},{25,17},{10,2},{18,10},{26,18},{... | collective-permute-start | bytes 737288 | tf_op jit(solution)/shard_map/while/body/eval_jaxpr/ppermute | solution.py:13
  165.8 14.5 %collective-permute-start = (f32[4,15360]{1,0:T(4,128)S(1)}, f32[4,15360]{1,0:T(4,128)S(1)}, u32[]{:S(2)}, u32[]{:S(2)}) collective-permute-start(f32[4,15360]{1,0:T(4,128)S(1)} %get-tuple-element.844), channel_id=1, source_target_pairs={{0,8},{8,16},{16,24},{1,9},{9,17},{17,25},{2,10},{10,18},{18,26},{... | collective-permute-start | bytes 737288 | tf_op jit(solution)/shard_map/while/body/eval_jaxpr/ppermute | solution.py:13
  175.8 114.5 %collective-permute-start.1 = (f32[4,15360]{1,0:T(4,128)S(1)}, f32[4,15360]{1,0:T(4,128)S(1)}, u32[]{:S(2)}, u32[]{:S(2)}) collective-permute-start(f32[4,15360]{1,0:T(4,128)S(1)} %get-tuple-element.845), channel_id=1, source_target_pairs={{8,0},{16,8},{24,16},{9,1},{17,9},{25,17},{10,2},{18,10},{26,18},{... | collective-permute-start | bytes 737288 | tf_op jit(solution)/shard_map/while/body/eval_jaxpr/ppermute | solution.py:13
  297.8 59.7 %collective-permute-start = (f32[4,15360]{1,0:T(4,128)S(1)}, f32[4,15360]{1,0:T(4,128)S(1)}, u32[]{:S(2)}, u32[]{:S(2)}) collective-permute-start(f32[4,15360]{1,0:T(4,128)S(1)} %get-tuple-element.844), channel_id=1, source_target_pairs={{0,8},{8,16},{16,24},{1,9},{9,17},{17,25},{2,10},{10,18},{18,26},{... | collective-permute-start | bytes 737288 | tf_op jit(solution)/shard_map/while/body/eval_jaxpr/ppermute | solution.py:13
  356.2 8.1 %collective-permute-start.1 = (f32[4,15360]{1,0:T(4,128)S(1)}, f32[4,15360]{1,0:T(4,128)S(1)}, u32[]{:S(2)}, u32[]{:S(2)}) collective-permute-start(f32[4,15360]{1,0:T(4,128)S(1)} %get-tuple-element.845), channel_id=1, source_target_pairs={{8,0},{16,8},{24,16},{9,1},{17,9},{25,17},{10,2},{18,10},{26,18},{... | collective-permute-start | bytes 737288 | tf_op jit(solution)/shard_map/while/body/eval_jaxpr/ppermute | solution.py:13
  367.8 4.2 %copy-start = (bf16[15,4,15360]{2,1,0:T(4,128)(2,1)S(1)}, bf16[15,4,15360]{2,1,0:T(4,128)(2,1)}, u32[]{:S(2)}) copy-start(bf16[15,4,15360]{2,1,0:T(4,128)(2,1)} %get-tuple-element.487) | copy-start | bytes 5529604
where the time goes:
time: 378 us; the launch traced here: 377 us
  waiting for transfers between devices  136 us (36%)
  starting transfers between devices  73 us (19%)
  local copies, waits for them, and re-layouts  61.5 us (16%)
  other arithmetic  56.1 us (15%)
  loops' own time  39.7 us (11%)
  blocking collectives  10.7 us (3%)
    ppermute x8, waiting for transfers between devices, passed_along(): lax.ppermute(value, axis, [(source, source + steps) for source in range(i...  136 us
    ppermute x8, starting transfers between devices, passed_along(): lax.ppermute(value, axis, [(source, source + steps) for source in range(i...  73 us
    shift_right_arithmetic x12, local copies, waits for them, and re-layouts, unpack_alleles(): jnp.right_shift(packed[:, :, None], shifts[None, None, :])  37.1 us
    dynamic_update_slice x30, other arithmetic, forward_pass(): return lax.scan(advance, state, (haplos, observed, rates))  22.3 us
    another operation x1, loops' own time, backward_pass(): return lax.scan(retreat, state, (haplos, observed, rates), reverse=True)  19.8 us
    another operation x1, loops' own time, forward_pass(): return lax.scan(advance, state, (haplos, observed, rates))  19.4 us
    dynamic_slice x30, local copies, waits for them, and re-layouts, forward_pass(): return lax.scan(advance, state, (haplos, observed, rates))  18.3 us
    all_gather x1, blocking collectives, local(): packed = lax.all_gather(alleles, 'hap', axis=1, tiled=True)  10.7 us
  transfers between devices with their start and end apart: 8, of which 7 were waited for; matrix products, arithmetic and copies ran while one was open for 9% of the time, Pallas kernels for 0%

commit v1 on v0

v1 whole, which is shorter than its diff:
```python
import functools
import jax
import jax.numpy as jnp
from jax import lax
from jax.experimental import pallas as pl
from jax.experimental.pallas import tpu as pltpu
from jax.sharding import PartitionSpec as P

error_rate = 0.01
map_unit = 100000.0
SUB, LANE = 8, 128
MESH = pl.DeviceIdType.MESH


def total(parts):
    parts = list(parts)
    while len(parts) > 1:
        parts = [a + b for a, b in zip(parts[::2], parts[1::2])] + parts[len(parts) // 2 * 2:]
    return parts[0]


def whole_sum(parts):
    return jnp.sum(total(parts), keepdims=True)


def kernel(dims, alleles, observed, steps, starts, ends, out, tmp, meta, sbuf, recv, recv_meta,
           bits, table, staged, fstore, bstore, numer, denom, dos, out_recv,
           send_sem, recv_sem, meta_send, meta_recv, out_send, out_recv_sem):
    groups, haps, local_m, targets, words, bits_word = dims
    total_haps = words * bits_word
    local_w = words // haps
    span = words // SUB
    reps = LANE // span
    vecs = bits_word // reps
    pack = LANE // local_w
    rows = -(-local_m // pack)
    slots = pack * rows
    share = haps // SUB
    half = groups // 2
    g_me, h_me = lax.axis_index("grp"), lax.axis_index("hap")
    devices = groups * haps
    me = g_me * haps + h_me
    mine = lax.rem(g_me, targets)

    barrier = pltpu.get_barrier_semaphore()

    @pl.loop(1, devices)
    def _(d):
        peer = lax.rem(me + d, devices)
        pl.semaphore_signal(barrier, inc=1, device_id=(peer // haps, lax.rem(peer, haps)), device_id_type=MESH)

    lane = lax.broadcasted_iota(jnp.int32, (SUB, LANE), 1)
    tmp[...] = jnp.zeros_like(tmp)
    tmp[0:local_m, 0:local_w] = alleles[...]
    dense = tmp[0:SUB, :]
    for p in range(1, pack):
        dense = jnp.where(lane // local_w == p, pltpu.roll(tmp[p * rows:p * rows + SUB, :], p * local_w, 1), dense)
    sbuf[...] = dense
    recv[g_me, pl.ds(pl.multiple_of(h_me * SUB, SUB), SUB), :] = dense
    meta[...] = jnp.zeros_like(meta)
    meta[0:local_m, 0:targets] = observed[...]
    row16 = lax.broadcasted_iota(jnp.int32, meta.shape, 0)
    lane16 = lax.broadcasted_iota(jnp.int32, meta.shape, 1)
    column = meta[...]
    for i in range(local_m):
        column = jnp.where((row16 == i) & (lane16 == targets), steps[i], column)
    meta[...] = column
    recv_meta[g_me] = column

    pl.semaphore_wait(barrier, devices - 1)

    def block_copy(g, h, sem_g, sem_h):
        return pltpu.make_async_remote_copy(
            src_ref=sbuf, dst_ref=recv.at[sem_g, pl.ds(pl.multiple_of(sem_h * SUB, SUB), SUB), :],
            send_sem=send_sem.at[g, h], recv_sem=recv_sem.at[sem_g, sem_h],
            device_id=(g, h), device_id_type=MESH)

    def meta_copy(g, sem_g):
        return pltpu.make_async_remote_copy(
            src_ref=meta, dst_ref=recv_meta.at[sem_g], send_sem=meta_send.at[g], recv_sem=meta_recv.at[sem_g],
            device_id=(g, h_me), device_id_type=MESH)

    @pl.loop(1, groups)
    def _(d):
        g = lax.rem(g_me + d, groups)
        meta_copy(g, g_me).start()

    @pl.loop(1, devices)
    def _(d):
        peer = lax.rem(me + d, devices)
        block_copy(peer // haps, lax.rem(peer, haps), g_me, h_me).start()

    def arrange(weights):
        for r in range(vecs):
            for s in range(SUB):
                at = s * vecs + r
                staged[at * targets:(at + 1) * targets, :] = weights[:, at * LANE:(at + 1) * LANE]
        source = [staged[pl.ds(r * targets + mine, SUB, stride=vecs * targets), :] for r in range(vecs)]
        result = []
        for q in range(vecs):
            spot = bits_word * (lane % span) + reps * q + lane // span
            chosen, within = spot // LANE, spot % LANE
            value = jnp.zeros((SUB, LANE), jnp.float32)
            for r in range(vecs):
                moved = jnp.take_along_axis(source[r], within, axis=1, mode="promise_in_bounds")
                value = jnp.where(chosen == r, moved, value)
            result.append(value)
        inverse = 1.0 / whole_sum(result)
        return [value * inverse for value in result]

    fwd = arrange(starts)
    bwd = arrange(ends)

    @pl.loop(1, groups)
    def _(d):
        meta_copy(g_me, lax.rem(g_me + d, groups)).wait_recv()

    @pl.loop(0, groups)
    def _(g):
        entry = recv_meta[g].astype(jnp.float32)
        seen = jnp.sum(jnp.where(lane16 == mine, entry, 0.0), axis=1, keepdims=True)
        dist = jnp.sum(jnp.where(lane16 == targets, entry, 0.0), axis=1, keepdims=True)
        seen = jnp.broadcast_to(seen, entry.shape)
        dist = jnp.broadcast_to(dist, entry.shape)
        rate = 1.0 - jnp.exp(-dist / map_unit)
        at = pl.ds(pl.multiple_of(g * slots, SUB), slots)
        table[0, at, :] = jnp.where(seen == 2.0, 1.0, jnp.where(seen == 1.0, 1.0 - error_rate, error_rate))
        table[1, at, :] = jnp.where(seen == 2.0, 1.0, jnp.where(seen == 0.0, 1.0 - error_rate, error_rate))
        table[2, at, :] = 1.0 - rate
        table[3, at, :] = rate / total_haps

    def expand(g):
        @pl.loop(0, haps)
        def _(h):
            @pl.when((g != g_me) | (h != h_me))
            def _():
                block_copy(g_me, h_me, g, h).wait_recv()

        for r in range(rows):
            loads = [recv[g, pl.ds(j * SUB + r, SUB, stride=SUB * share), :] for j in range(share)]
            for p in range(pack):
                value = jnp.zeros((SUB, LANE), jnp.int32)
                for e in range(reps):
                    for j in range(share):
                        begin = e * span + j * local_w
                        shift = (begin - p * local_w) % LANE
                        piece = loads[j] if shift == 0 else pltpu.roll(loads[j], shift, 1)
                        piece = piece if e == 0 else jnp.right_shift(piece, e)
                        value = jnp.where((lane >= begin) & (lane < begin + local_w), piece, value)
                bits[g * slots + p * rows + r] = value

    def row(kind, slot):
        return jnp.broadcast_to(table[kind, pl.ds(slot, 1), :], (SUB, LANE))

    def emitted(slot):
        word = bits[slot]
        one, zero = row(0, slot), row(1, slot)
        return [jnp.where(jnp.bitwise_and(word, 1 << (reps * q)) != 0, one, zero) for q in range(vecs)]

    def rounded(values):
        return [value.astype(jnp.bfloat16).astype(jnp.float32) for value in values]

    def move_forward(f, slot):
        keep, add = row(2, slot), row(3, slot)
        w = [e * (keep * v + add) for e, v in zip(emitted(slot), f)]
        inverse = 1.0 / whole_sum(w)
        return [v * inverse for v in w]

    def move_backward(b, slot):
        w = [e * v for e, v in zip(emitted(slot), b)]
        keep, add = row(2, slot) / whole_sum(w), row(3, slot)
        return [keep * v + add for v in w]

    def store_section(s, carry):
        expand(s)
        expand(groups - 1 - s)

        def step(i, carry):
            f, b = list(carry[:vecs]), list(carry[vecs:])
            fs, bs = s * slots + i, (groups - 1 - s) * slots + local_m - 1 - i
            f = move_forward(f, fs)
            for q in range(vecs):
                fstore[s * local_m + i, q] = f[q]
                bstore[s * local_m + i, q] = b[q]
            b = move_backward(b, bs)
            return tuple(f) + tuple(b)

        return lax.fori_loop(0, local_m, step, carry)

    def score(f, b, slot):
        word = bits[slot]
        prod = [x * y for x, y in zip(rounded(f), rounded(b))]
        numer[slot] = total([jnp.where(jnp.bitwise_and(word, 1 << (reps * q)) != 0, v, 0.0) for q, v in enumerate(prod)])
        denom[slot] = total(prod)

    def score_section(s, carry):
        def step(i, carry):
            f, b = list(carry[:vecs]), list(carry[vecs:])
            fs, bs = s * slots + i, (groups - 1 - s) * slots + local_m - 1 - i
            other = (groups - 1 - s) * local_m + local_m - 1 - i
            score([fstore[other, q] for q in range(vecs)], b, bs)
            f = move_forward(f, fs)
            score(f, [bstore[other, q] for q in range(vecs)], fs)
            b = move_backward(b, bs)
            return tuple(f) + tuple(b)

        return lax.fori_loop(0, local_m, step, carry)

    carry = lax.fori_loop(0, half, store_section, tuple(fwd) + tuple(bwd))
    lax.fori_loop(half, groups, score_section, carry)

    def out_copy(g, owner):
        return pltpu.make_async_remote_copy(
            src_ref=dos.at[g], dst_ref=out_recv.at[owner], send_sem=out_send.at[g],
            recv_sem=out_recv_sem.at[owner], device_id=(g, h_me), device_id_type=MESH)

    owner = g_me < targets

    @pl.loop(0, groups)
    def _(g):
        at = pl.ds(g * slots, local_m)
        top = jnp.sum(jnp.sum(numer[at], axis=1), axis=1, keepdims=True)
        low = jnp.sum(jnp.sum(denom[at], axis=1), axis=1, keepdims=True)
        dos[g, 0:local_m, :] = jnp.broadcast_to(top / low, (local_m, LANE))

        @pl.when((g != g_me) & owner)
        def _():
            out_copy(g, g_me).start()

    @pl.when(owner)
    def _():
        out_recv[g_me, 0:local_m, :] = dos[g_me, 0:local_m, :]

    @pl.loop(0, targets)
    def _(t):
        @pl.when(t != g_me)
        def _():
            out_copy(g_me, t).wait_recv()

    lane_m = lax.broadcasted_iota(jnp.int32, (local_m, LANE), 1)
    result = jnp.zeros((local_m, LANE), jnp.float32)
    for t in range(targets):
        result = jnp.where(lane_m == t, out_recv[t, 0:local_m, :], result)
    out[...] = result[:, 0:targets]

    @pl.loop(1, groups)
    def _(d):
        g = lax.rem(g_me + d, groups)
        meta_copy(g, g_me).wait_send()

        @pl.when(owner)
        def _():
            out_copy(g, g_me).wait_send()

    @pl.loop(1, devices)
    def _(d):
        peer = lax.rem(me + d, devices)
        block_copy(peer // haps, lax.rem(peer, haps), g_me, h_me).wait_send()


def solution(mesh):
    groups, haps = mesh.shape["grp"], mesh.shape["hap"]

    def local(alleles, observed, map_steps, start_weights, end_weights):
        local_m, local_w = alleles.shape
        targets, total_haps = start_weights.shape
        words = local_w * haps
        bits_word = total_haps // words
        reps = LANE * SUB // words
        vecs = bits_word // reps
        pack = LANE // local_w
        slots = pack * -(-local_m // pack)
        markers = local_m * groups
        assert targets <= groups and groups % 2 == 0 and slots % SUB == 0
        vmem = pl.BlockSpec(memory_space=pltpu.VMEM)
        dims = (groups, haps, local_m, targets, words, bits_word)
        f32, i32 = jnp.float32, jnp.int32
        dma = pltpu.SemaphoreType.DMA
        return pl.pallas_call(
            functools.partial(kernel, dims),
            out_shape=jax.ShapeDtypeStruct((local_m, targets), f32),
            in_specs=[vmem, vmem, pl.BlockSpec(memory_space=pltpu.SMEM), vmem, vmem],
            out_specs=vmem,
            scratch_shapes=[
                pltpu.VMEM((slots + SUB, LANE), i32),
                pltpu.VMEM((slots, LANE), i32),
                pltpu.VMEM((SUB, LANE), i32),
                pltpu.VMEM((groups, haps * SUB, LANE), i32),
                pltpu.VMEM((groups, slots, LANE), i32),
                pltpu.VMEM((groups * slots, SUB, LANE), i32),
                pltpu.VMEM((4, groups * slots, LANE), f32),
                pltpu.VMEM((vecs * SUB * targets, LANE), f32),
                pltpu.VMEM((markers // 2, vecs, SUB, LANE), f32),
                pltpu.VMEM((markers // 2, vecs, SUB, LANE), f32),
                pltpu.VMEM((groups * slots, SUB, LANE), f32),
                pltpu.VMEM((groups * slots, SUB, LANE), f32),
                pltpu.VMEM((groups, slots, LANE), f32),
                pltpu.VMEM((targets, slots, LANE), f32),
                dma((groups, haps)), dma((groups, haps)),
                dma((groups,)), dma((groups,)), dma((groups,)), dma((targets,)),
            ],
            compiler_params=pltpu.CompilerParams(
                collective_id=0, has_side_effects=True, vmem_limit_bytes=48 * 1024 * 1024),
        )(alleles, observed, map_steps, start_weights, end_weights)

    in_specs = (P("grp", "hap"), P("grp", "hap"), P("grp"), P("hap", None), P("hap", None))
    return jax.shard_map(local, mesh=mesh, in_specs=in_specs, out_specs=P("grp", "hap"), check_vma=False)
```

time: 378 us -> 31.9 us (0.08)
  waiting for transfers between devices: 136 us -> 0 us
  starting transfers between devices: 73 us -> 0 us
  local copies, waits for them, and re-layouts: 61.5 us -> 3.35 us
  other arithmetic: 56.1 us -> 0 us
  loops' own time: 39.7 us -> 0 us
  Pallas kernels: 0 us -> 28.3 us
  blocking collectives: 10.7 us -> 0 us
    ppermute x8 -> x0, waiting for transfers between devices: 136 us -> none  [passed_along(): lax.ppermute(value, axis, [(source, source + steps) for source in range(i...]
    ppermute x8 -> x0, starting transfers between devices: 73 us -> none  [passed_along(): lax.ppermute(value, axis, [(source, source + steps) for source in range(i...]
    another operation x11 -> x0, loops' own time: 39.7 us -> none  [the longest x1 19.8 us: backward_pass(): return lax.scan(retreat, state, (haplos, observed, rates), reverse=True)]
    shift_right_arithmetic x12 -> x0, local copies, waits for them, and re-layouts: 37.1 us -> none  [unpack_alleles(): jnp.right_shift(packed[:, :, None], shifts[None, None, :])]
    pallas_call x0 -> x1, Pallas kernels: none -> 28.3 us  [local(): pl.pallas_call(functools.partial(kernel, dims), out_shape=jax.ShapeDtypeS...]
    dynamic_update_slice x30 -> x0, other arithmetic: 22.3 us -> none  [forward_pass(): return lax.scan(advance, state, (haplos, observed, rates))]
    reduce_sum x62 -> x0, other arithmetic: 21.9 us -> none  [the longest x15 5.88 us: advance(): weighted = weighted / jnp.sum(weighted, axis=1, keepdims=True)]
    dynamic_slice x30 -> x0, local copies, waits for them, and re-layouts: 18.3 us -> none  [forward_pass(): return lax.scan(advance, state, (haplos, observed, rates))]
  transfers between devices with their start and end apart: 8 -> 0, of which waited for: 7 -> 0; matrix products, arithmetic and copies ran while one was open for 9% -> 0% of each run, Pallas kernels for 0% -> 0%
where the time goes in v1:
time: 31.9 us; the launch traced here: 31.7 us
  Pallas kernels  28.3 us (89%)
  local copies, waits for them, and re-layouts  3.35 us (11%)
    pallas_call x1, Pallas kernels, local(): pl.pallas_call(functools.partial(kernel, dims), out_shape=jax.ShapeDtypeS...  28.3 us
    unnamed x9, local copies, waits for them, and re-layouts  2.69 us
    pallas_call x1, local copies, waits for them, and re-layouts, local(): pl.pallas_call(functools.partial(kernel, dims), out_shape=jax.ShapeDtypeS...  0.66 us

profile of v1, /device:TPU:0, one launch (start us, length us, event | category | flops | bytes accessed | tf_op | source)
XLA Modules:
  0.0 31.7 jit_solution(10708731966206422358)
XLA Ops:
  0.0 0.0 copy-start.3
  0.0 0.0 copy-start.2
  0.0 0.8 %copy.6.observed = s32[15,4]{1,0:T(8,128)S(1)} copy(s32[15,4]{0,1:T(4,128)} %param.6) | data formatting | bytes 480 | tf_op args[1]
  0.8 0.0 copy-done.3
  0.8 0.0 copy-done.2
  0.8 0.0 copy-start
  0.8 0.9 %copy-done = f32[4,15360]{1,0:T(4,128)S(1)} copy-done((f32[4,15360]{1,0:T(4,128)S(1)}, f32[4,15360]{1,0:T(4,128)}, u32[]{:S(2)}) %copy-start) | copy-done | bytes 245784
  1.8 0.0 copy-start.1
  1.8 0.9 %copy-done.1 = f32[4,15360]{1,0:T(4,128)S(1)} copy-done((f32[4,15360]{1,0:T(4,128)S(1)}, f32[4,15360]{1,0:T(4,128)}, u32[]{:S(2)}) %copy-start.1) | copy-done | bytes 245784
  2.7 28.3 %shard_map.55 = f32[15,4]{1,0:T(8,128)S(1)} custom-call(s32[15,64]{1,0:T(8,128)S(1)} %copy-done.2, s32[15,4]{1,0:T(8,128)S(1)} %copy.6.observed, s32[15]{0:T(128)S(1)} %copy-done.3, f32[4,15360]{1,0:T(4,128)S(1)} %copy-done, f32[4,15360]{1,0:T(4,128)S(1)} %copy-done.1), custom_call_target="tpu_custom_call" | custom-call | tf_op jit(solution)/shard_map/pallas_call | solution.py:279
  31.0 0.7 %copy.7 = f32[15,4]{0,1:T(4,128)} copy(f32[15,4]{1,0:T(8,128)S(1)} %shard_map.55) | data formatting | bytes 480 | tf_op jit(solution)/shard_map/pallas_call | solution.py:279
Async XLA Ops:
  0.0 0.8 %copy-start.3 = (s32[15]{0:T(128)S(1)}, s32[15]{0:T(128)}, u32[]{:S(2)}) copy-start(s32[15]{0:T(128)} %steps.1) | copy-start | bytes 184
  0.0 0.8 %copy-start.2 = (s32[15,64]{1,0:T(8,128)S(1)}, s32[15,64]{1,0:T(8,128)}, u32[]{:S(2)}) copy-start(s32[15,64]{1,0:T(8,128)} %alleles.1) | copy-start | bytes 11524
  0.8 0.9 %copy-start = (f32[4,15360]{1,0:T(4,128)S(1)}, f32[4,15360]{1,0:T(4,128)}, u32[]{:S(2)}) copy-start(f32[4,15360]{1,0:T(4,128)} %starts.1) | copy-start | bytes 737284
  1.8 0.9 %copy-start.1 = (f32[4,15360]{1,0:T(4,128)S(1)}, f32[4,15360]{1,0:T(4,128)}, u32[]{:S(2)}) copy-start(f32[4,15360]{1,0:T(4,128)} %ends.1) | copy-start | bytes 737284

commit v2 on v1

--- a/solution.py
+++ b/solution.py
@@ -19,12 +19,16 @@
     return parts[0]
 
 
+def block_size(local_m):
+    return next(n for n in (5, 4, 3, 2, 1) if local_m % n == 0)
+
+
 def whole_sum(parts):
     return jnp.sum(total(parts), keepdims=True)
 
 
 def kernel(dims, alleles, observed, steps, starts, ends, out, tmp, meta, sbuf, recv, recv_meta,
-           bits, table, staged, fstore, bstore, numer, denom, dos, out_recv,
+           bits, table, staged, fstore, bstore, emit, runs, numer, denom, dos, out_recv,
            send_sem, recv_sem, meta_send, meta_recv, out_send, out_recv_sem):
     groups, haps, local_m, targets, words, bits_word = dims
     total_haps = words * bits_word
@@ -37,6 +41,7 @@
     slots = pack * rows
     share = haps // SUB
     half = groups // 2
+    size = block_size(local_m)
     g_me, h_me = lax.axis_index("grp"), lax.axis_index("hap")
     devices = groups * haps
     me = g_me * haps + h_me
@@ -67,29 +72,6 @@
     meta[...] = column
     recv_meta[g_me] = column
 
-    pl.semaphore_wait(barrier, devices - 1)
-
-    def block_copy(g, h, sem_g, sem_h):
-        return pltpu.make_async_remote_copy(
-            src_ref=sbuf, dst_ref=recv.at[sem_g, pl.ds(pl.multiple_of(sem_h * SUB, SUB), SUB), :],
-            send_sem=send_sem.at[g, h], recv_sem=recv_sem.at[sem_g, sem_h],
-            device_id=(g, h), device_id_type=MESH)
-
-    def meta_copy(g, sem_g):
-        return pltpu.make_async_remote_copy(
-            src_ref=meta, dst_ref=recv_meta.at[sem_g], send_sem=meta_send.at[g], recv_sem=meta_recv.at[sem_g],
-            device_id=(g, h_me), device_id_type=MESH)
-
-    @pl.loop(1, groups)
-    def _(d):
-        g = lax.rem(g_me + d, groups)
-        meta_copy(g, g_me).start()
-
-    @pl.loop(1, devices)
-    def _(d):
-        peer = lax.rem(me + d, devices)
-        block_copy(peer // haps, lax.rem(peer, haps), g_me, h_me).start()
-
     def arrange(weights):
         for r in range(vecs):
             for s in range(SUB):
@@ -109,6 +91,30 @@
         return [value * inverse for value in result]
 
     fwd = arrange(starts)
+
+    pl.semaphore_wait(barrier, devices - 1)
+
+    def block_copy(g, h, sem_g, sem_h):
+        return pltpu.make_async_remote_copy(
+            src_ref=sbuf, dst_ref=recv.at[sem_g, pl.ds(pl.multiple_of(sem_h * SUB, SUB), SUB), :],
+            send_sem=send_sem.at[g, h], recv_sem=recv_sem.at[sem_g, sem_h],
+            device_id=(g, h), device_id_type=MESH)
+
+    def meta_copy(g, sem_g):
+        return pltpu.make_async_remote_copy(
+            src_ref=meta, dst_ref=recv_meta.at[sem_g], send_sem=meta_send.at[g], recv_sem=meta_recv.at[sem_g],
+            device_id=(g, h_me), device_id_type=MESH)
+
+    @pl.loop(1, groups)
+    def _(d):
+        g = lax.rem(g_me + d, groups)
+        meta_copy(g, g_me).start()
+
+    @pl.loop(1, devices)
+    def _(d):
+        peer = lax.rem(me + d, devices)
+        block_copy(peer // haps, lax.rem(peer, haps), g_me, h_me).start()
+
     bwd = arrange(ends)
 
     @pl.loop(1, groups)
@@ -152,59 +158,138 @@
     def row(kind, slot):
         return jnp.broadcast_to(table[kind, pl.ds(slot, 1), :], (SUB, LANE))
 
-    def emitted(slot):
-        word = bits[slot]
-        one, zero = row(0, slot), row(1, slot)
-        return [jnp.where(jnp.bitwise_and(word, 1 << (reps * q)) != 0, one, zero) for q in range(vecs)]
-
-    def rounded(values):
-        return [value.astype(jnp.bfloat16).astype(jnp.float32) for value in values]
-
-    def move_forward(f, slot):
-        keep, add = row(2, slot), row(3, slot)
-        w = [e * (keep * v + add) for e, v in zip(emitted(slot), f)]
-        inverse = 1.0 / whole_sum(w)
-        return [v * inverse for v in w]
-
-    def move_backward(b, slot):
-        w = [e * v for e, v in zip(emitted(slot), b)]
-        keep, add = row(2, slot) / whole_sum(w), row(3, slot)
-        return [keep * v + add for v in w]
+    def add_up(value):
+        return jnp.broadcast_to(jnp.sum(value, keepdims=True), (SUB, LANE))
+
+    pairs = [(j, i) for j in range(size) for i in range(j, size)]
+
+    def spans(slot, block):
+        sums = {pair: [] for pair in pairs}
+        words_in = [bits[slot + i] for i in range(size)]
+        tops = [(row(0, slot + i), row(1, slot + i)) for i in range(size)]
+        for q in range(vecs):
+            e = [jnp.where(jnp.bitwise_and(words_in[i], 1 << (reps * q)) != 0, *tops[i]) for i in range(size)]
+            for i in range(size):
+                emit[slot + i, q] = e[i]
+            for j in range(size):
+                run = e[j]
+                for i in range(j, size):
+                    run = run if i == j else run * e[i]
+                    sums[j, i] = [run] if q == 0 else [sums[j, i][0] + run]
+        result = {}
+        for at, pair in enumerate(pairs):
+            result[pair] = add_up(sums[pair][0])
+            runs[block, at] = result[pair]
+        return result
+
+    def kept_spans(block):
+        return {pair: runs[block, at] for at, pair in enumerate(pairs)}
+
+    def ahead(state, order):
+        sums = [None] * size
+        for q in range(vecs):
+            value = state[q]
+            for i, slot in enumerate(order):
+                value = value * emit[slot, q]
+                sums[i] = value if q == 0 else sums[i] + value
+        return [add_up(value) for value in sums]
+
+    def solve_forward(first, span, order):
+        keep = [row(2, slot) for slot in order]
+        add = [row(3, slot) for slot in order]
+        sums, terms = [], []
+        lead = None
+        for i in range(size):
+            lead = keep[i] if i == 0 else lead * keep[i]
+            terms = [term * keep[i] for term in terms]
+            terms.append(add[i] if i == 0 else add[i] * sums[i - 1])
+            value = lead * first[i]
+            for j, term in enumerate(terms):
+                value = value + term * span[j, i]
+            sums.append(value)
+        scale = [(1.0 if i == 0 else sums[i - 1]) / sums[i] for i in range(size)]
+        return [keep[i] * scale[i] for i in range(size)], [add[i] * scale[i] for i in range(size)]
+
+    def solve_backward(first, span, order):
+        keep = [row(2, slot) for slot in order]
+        add = [row(3, slot) for slot in order]
+        sums, terms = [], []
+        lead = None
+        for i in range(size):
+            value = first[i] if i == 0 else lead * first[i]
+            for j, term in enumerate(terms):
+                value = value + term * span[size - 1 - i, size - 2 - j]
+            sums.append(value)
+            lead = keep[i] if i == 0 else lead * keep[i]
+            terms = [term * keep[i] for term in terms] + [add[i] * value]
+        scale = [(1.0 if i == 0 else sums[i - 1]) / sums[i] for i in range(size)]
+        return [keep[i] * scale[i] for i in range(size)], add
+
+    blocks = local_m // size
+
+    def place(s, n):
+        slot = s * slots + n * size
+        return slot, s * local_m + n * size, s * blocks + n
 
     def store_section(s, carry):
         expand(s)
         expand(groups - 1 - s)
 
-        def step(i, carry):
+        def step(n, carry):
             f, b = list(carry[:vecs]), list(carry[vecs:])
-            fs, bs = s * slots + i, (groups - 1 - s) * slots + local_m - 1 - i
-            f = move_forward(f, fs)
+            fs, fm, fb = place(s, n)
+            bs, _, bb = place(groups - 1 - s, blocks - 1 - n)
+            bm = s * local_m + n * size
+            f_order = [fs + i for i in range(size)]
+            b_order = [bs + size - 1 - i for i in range(size)]
+            f_span, b_span = spans(fs, fb), spans(bs, bb)
+            f_first, b_first = ahead(f, f_order), ahead(b, b_order)
+            f_keep, f_add = solve_forward(f_first, f_span, f_order)
+            b_keep, b_add = solve_backward(b_first, b_span, b_order)
             for q in range(vecs):
-                fstore[s * local_m + i, q] = f[q]
-                bstore[s * local_m + i, q] = b[q]
-            b = move_backward(b, bs)
+                for i in range(size):
+                    f[q] = emit[f_order[i], q] * (f_keep[i] * f[q] + f_add[i])
+                    fstore[fm + i, q] = f[q]
+                    bstore[bm + i, q] = b[q]
+                    b[q] = b_keep[i] * (emit[b_order[i], q] * b[q]) + b_add[i]
             return tuple(f) + tuple(b)
 
-        return lax.fori_loop(0, local_m, step, carry)
-
-    def score(f, b, slot):
-        word = bits[slot]
-        prod = [x * y for x, y in zip(rounded(f), rounded(b))]
-        numer[slot] = total([jnp.where(jnp.bitwise_and(word, 1 << (reps * q)) != 0, v, 0.0) for q, v in enumerate(prod)])
-        denom[slot] = total(prod)
+        return lax.fori_loop(0, blocks, step, carry)
+
+    def half_type(value):
+        return value.astype(jnp.bfloat16).astype(jnp.float32)
 
     def score_section(s, carry):
-        def step(i, carry):
+        def step(n, carry):
             f, b = list(carry[:vecs]), list(carry[vecs:])
-            fs, bs = s * slots + i, (groups - 1 - s) * slots + local_m - 1 - i
-            other = (groups - 1 - s) * local_m + local_m - 1 - i
-            score([fstore[other, q] for q in range(vecs)], b, bs)
-            f = move_forward(f, fs)
-            score(f, [bstore[other, q] for q in range(vecs)], fs)
-            b = move_backward(b, bs)
+            fs, _, fb = place(s, n)
+            bs, _, bb = place(groups - 1 - s, blocks - 1 - n)
+            other = (groups - 1 - s) * local_m + local_m - 1 - n * size
+            f_order = [fs + i for i in range(size)]
+            b_order = [bs + size - 1 - i for i in range(size)]
+            f_first, b_first = ahead(f, f_order), ahead(b, b_order)
+            f_keep, f_add = solve_forward(f_first, kept_spans(fb), f_order)
+            b_keep, b_add = solve_backward(b_first, kept_spans(bb), b_order)
+            tops, lows = {}, {}
+
+            def score(key, q, x, y, slot):
+                prod = half_type(x) * half_type(y)
+                part = jnp.where(jnp.bitwise_and(bits[slot], 1 << (reps * q)) != 0, prod, 0.0)
+                tops[key] = part if q == 0 else tops[key] + part
+                lows[key] = prod if q == 0 else lows[key] + prod
+
+            for q in range(vecs):
+                for i in range(size):
+                    f[q] = emit[f_order[i], q] * (f_keep[i] * f[q] + f_add[i])
+                    score((0, i), q, f[q], bstore[other - i, q], f_order[i])
+                    score((1, i), q, fstore[other - i, q], b[q], b_order[i])
+                    b[q] = b_keep[i] * (emit[b_order[i], q] * b[q]) + b_add[i]
+            for i in range(size):
+                numer[f_order[i]], denom[f_order[i]] = tops[0, i], lows[0, i]
+                numer[b_order[i]], denom[b_order[i]] = tops[1, i], lows[1, i]
             return tuple(f) + tuple(b)
 
-        return lax.fori_loop(0, local_m, step, carry)
+        return lax.fori_loop(0, blocks, step, carry)
 
     carry = lax.fori_loop(0, half, store_section, tuple(fwd) + tuple(bwd))
     lax.fori_loop(half, groups, score_section, carry)
@@ -216,7 +301,7 @@
 
     owner = g_me < targets
 
-    @pl.loop(0, groups)
+    @pl.loop(0, groups, unroll=min(groups, 4))
     def _(g):
         at = pl.ds(g * slots, local_m)
         top = jnp.sum(jnp.sum(numer[at], axis=1), axis=1, keepdims=True)
@@ -271,6 +356,7 @@
         pack = LANE // local_w
         slots = pack * -(-local_m // pack)
         markers = local_m * groups
+        size = block_size(local_m)
         assert targets <= groups and groups % 2 == 0 and slots % SUB == 0
         vmem = pl.BlockSpec(memory_space=pltpu.VMEM)
         dims = (groups, haps, local_m, targets, words, bits_word)
@@ -292,6 +378,8 @@
                 pltpu.VMEM((vecs * SUB * targets, LANE), f32),
                 pltpu.VMEM((markers // 2, vecs, SUB, LANE), f32),
                 pltpu.VMEM((markers // 2, vecs, SUB, LANE), f32),
+                pltpu.VMEM((groups * slots, vecs, SUB, LANE), f32),
+                pltpu.VMEM((markers // size, size * (size + 1) // 2, SUB, LANE), f32),
                 pltpu.VMEM((groups * slots, SUB, LANE), f32),
                 pltpu.VMEM((groups * slots, SUB, LANE), f32),
                 pltpu.VMEM((groups, slots, LANE), f32),

time: 31.9 us -> 27 us (0.85)
  Pallas kernels: 28.3 us -> 23.4 us
    pallas_call x1, Pallas kernels: 28.3 us -> 23.4 us  [local(): pl.pallas_call(functools.partial(kernel, dims), out_shape=jax.ShapeDtypeS...]
where the time goes in v2:
time: 27 us; the launch traced here: 26.8 us
  Pallas kernels  23.4 us (87%)
  local copies, waits for them, and re-layouts  3.35 us (12%)
    pallas_call x1, Pallas kernels, local(): pl.pallas_call(functools.partial(kernel, dims), out_shape=jax.ShapeDtypeS...  23.4 us
    unnamed x9, local copies, waits for them, and re-layouts  2.69 us
    pallas_call x1, local copies, waits for them, and re-layouts, local(): pl.pallas_call(functools.partial(kernel, dims), out_shape=jax.ShapeDtypeS...  0.66 us

profile of v2, /device:TPU:0, one launch (start us, length us, event | category | flops | bytes accessed | tf_op | source)
XLA Modules:
  0.0 26.8 jit_solution(2676653165479417904)
XLA Ops:
  0.0 0.0 copy-start.3
  0.0 0.0 copy-start.2
  0.0 0.8 %copy.6.observed = s32[15,4]{1,0:T(8,128)S(1)} copy(s32[15,4]{0,1:T(4,128)} %param.6) | data formatting | bytes 480 | tf_op args[1]
  0.8 0.0 copy-done.3
  0.8 0.0 copy-done.2
  0.8 0.0 copy-start
  0.8 0.9 %copy-done = f32[4,15360]{1,0:T(4,128)S(1)} copy-done((f32[4,15360]{1,0:T(4,128)S(1)}, f32[4,15360]{1,0:T(4,128)}, u32[]{:S(2)}) %copy-start) | copy-done | bytes 245784
  1.8 0.0 copy-start.1
  1.8 0.9 %copy-done.1 = f32[4,15360]{1,0:T(4,128)S(1)} copy-done((f32[4,15360]{1,0:T(4,128)S(1)}, f32[4,15360]{1,0:T(4,128)}, u32[]{:S(2)}) %copy-start.1) | copy-done | bytes 245784
  2.7 23.4 %shard_map.55 = f32[15,4]{1,0:T(8,128)S(1)} custom-call(s32[15,64]{1,0:T(8,128)S(1)} %copy-done.2, s32[15,4]{1,0:T(8,128)S(1)} %copy.6.observed, s32[15]{0:T(128)S(1)} %copy-done.3, f32[4,15360]{1,0:T(4,128)S(1)} %copy-done, f32[4,15360]{1,0:T(4,128)S(1)} %copy-done.1), custom_call_target="tpu_custom_call" | custom-call | tf_op jit(solution)/shard_map/pallas_call | solution.py:365
  26.1 0.7 %copy.7 = f32[15,4]{0,1:T(4,128)} copy(f32[15,4]{1,0:T(8,128)S(1)} %shard_map.55) | data formatting | bytes 480 | tf_op jit(solution)/shard_map/pallas_call | solution.py:365
Async XLA Ops:
  0.0 0.8 %copy-start.3 = (s32[15]{0:T(128)S(1)}, s32[15]{0:T(128)}, u32[]{:S(2)}) copy-start(s32[15]{0:T(128)} %steps.1) | copy-start | bytes 184
  0.0 0.8 %copy-start.2 = (s32[15,64]{1,0:T(8,128)S(1)}, s32[15,64]{1,0:T(8,128)}, u32[]{:S(2)}) copy-start(s32[15,64]{1,0:T(8,128)} %alleles.1) | copy-start | bytes 11524
  0.8 0.9 %copy-start = (f32[4,15360]{1,0:T(4,128)S(1)}, f32[4,15360]{1,0:T(4,128)}, u32[]{:S(2)}) copy-start(f32[4,15360]{1,0:T(4,128)} %starts.1) | copy-start | bytes 737284
  1.8 0.9 %copy-start.1 = (f32[4,15360]{1,0:T(4,128)S(1)}, f32[4,15360]{1,0:T(4,128)}, u32[]{:S(2)}) copy-start(f32[4,15360]{1,0:T(4,128)} %ends.1) | copy-start | bytes 737284

commit v3 on v2

--- a/solution.py
+++ b/solution.py
@@ -29,7 +29,7 @@
 
 def kernel(dims, alleles, observed, steps, starts, ends, out, tmp, meta, sbuf, recv, recv_meta,
            bits, table, staged, fstore, bstore, emit, runs, numer, denom, dos, out_recv,
-           send_sem, recv_sem, meta_send, meta_recv, out_send, out_recv_sem):
+           start_rows, end_rows, weight_sem, send_sem, recv_sem, meta_send, meta_recv, out_send, out_recv_sem):
     groups, haps, local_m, targets, words, bits_word = dims
     total_haps = words * bits_word
     local_w = words // haps
@@ -44,15 +44,35 @@
     size = block_size(local_m)
     g_me, h_me = lax.axis_index("grp"), lax.axis_index("hap")
     devices = groups * haps
-    me = g_me * haps + h_me
     mine = lax.rem(g_me, targets)
 
+    weight_copies = [
+        pltpu.make_async_copy(source, target, weight_sem.at[n])
+        for n, (source, target) in enumerate([(starts, start_rows), (ends, end_rows)])
+    ]
+    for copy in weight_copies:
+        copy.start()
+
+    def each_peer(act):
+        def visit(k, d):
+            g = jnp.where(g_me < half, groups - 1 - k, k)
+            h = lax.rem(h_me + d, haps)
+            if isinstance(d, int) and d:
+                act(g, h)
+            else:
+                pl.when((g != g_me) | (h != h_me))(lambda: act(g, h))
+
+        if devices <= 64:
+            for k in range(groups):
+                for d in range(haps):
+                    visit(k, d)
+        else:
+            @pl.loop(0, groups)
+            def _(k):
+                pl.loop(0, haps)(functools.partial(visit, k))
+
     barrier = pltpu.get_barrier_semaphore()
-
-    @pl.loop(1, devices)
-    def _(d):
-        peer = lax.rem(me + d, devices)
-        pl.semaphore_signal(barrier, inc=1, device_id=(peer // haps, lax.rem(peer, haps)), device_id_type=MESH)
+    each_peer(lambda g, h: pl.semaphore_signal(barrier, inc=1, device_id=(g, h), device_id_type=MESH))
 
     lane = lax.broadcasted_iota(jnp.int32, (SUB, LANE), 1)
     tmp[...] = jnp.zeros_like(tmp)
@@ -63,14 +83,13 @@
     sbuf[...] = dense
     recv[g_me, pl.ds(pl.multiple_of(h_me * SUB, SUB), SUB), :] = dense
     meta[...] = jnp.zeros_like(meta)
-    meta[0:local_m, 0:targets] = observed[...]
-    row16 = lax.broadcasted_iota(jnp.int32, meta.shape, 0)
-    lane16 = lax.broadcasted_iota(jnp.int32, meta.shape, 1)
-    column = meta[...]
+    meta[0:targets, 0:local_m] = observed[...]
+    columns = meta[...]
+    sub_at = lax.broadcasted_iota(jnp.int32, (SUB, LANE), 0)
     for i in range(local_m):
-        column = jnp.where((row16 == i) & (lane16 == targets), steps[i], column)
-    meta[...] = column
-    recv_meta[g_me] = column
+        columns = jnp.where((sub_at == targets) & (lane == i), steps[i], columns)
+    meta[...] = columns
+    recv_meta[g_me] = columns
 
     def arrange(weights):
         for r in range(vecs):
@@ -90,7 +109,8 @@
         inverse = 1.0 / whole_sum(result)
         return [value * inverse for value in result]
 
-    fwd = arrange(starts)
+    weight_copies[0].wait()
+    fwd = arrange(start_rows)
 
     pl.semaphore_wait(barrier, devices - 1)
 
@@ -110,12 +130,14 @@
         g = lax.rem(g_me + d, groups)
         meta_copy(g, g_me).start()
 
-    @pl.loop(1, devices)
-    def _(d):
-        peer = lax.rem(me + d, devices)
-        block_copy(peer // haps, lax.rem(peer, haps), g_me, h_me).start()
-
-    bwd = arrange(ends)
+    def send_blocks():
+        each_peer(lambda g, h: block_copy(g, h, g_me, h_me).start())
+
+    outer = (g_me == 0) | (g_me == groups - 1)
+    pl.when(outer)(send_blocks)
+    weight_copies[1].wait()
+    bwd = arrange(end_rows)
+    pl.when(jnp.logical_not(outer))(send_blocks)
 
     @pl.loop(1, groups)
     def _(d):
@@ -123,11 +145,15 @@
 
     @pl.loop(0, groups)
     def _(g):
-        entry = recv_meta[g].astype(jnp.float32)
-        seen = jnp.sum(jnp.where(lane16 == mine, entry, 0.0), axis=1, keepdims=True)
-        dist = jnp.sum(jnp.where(lane16 == targets, entry, 0.0), axis=1, keepdims=True)
-        seen = jnp.broadcast_to(seen, entry.shape)
-        dist = jnp.broadcast_to(dist, entry.shape)
+        entry = recv_meta.at[g]
+        same = lax.broadcasted_iota(jnp.int32, (slots, LANE), 0) == lax.broadcasted_iota(jnp.int32, (slots, LANE), 1)
+
+        def turned(at):
+            values = jnp.broadcast_to(entry[pl.ds(at, 1), :].astype(jnp.float32), (slots, LANE))
+            summed = jnp.sum(jnp.where(same, values, 0.0), axis=1, keepdims=True)
+            return jnp.broadcast_to(summed, (slots, LANE))
+
+        seen, dist = turned(mine), turned(targets)
         rate = 1.0 - jnp.exp(-dist / map_unit)
         at = pl.ds(pl.multiple_of(g * slots, SUB), slots)
         table[0, at, :] = jnp.where(seen == 2.0, 1.0, jnp.where(seen == 1.0, 1.0 - error_rate, error_rate))
@@ -159,7 +185,9 @@
         return jnp.broadcast_to(table[kind, pl.ds(slot, 1), :], (SUB, LANE))
 
     def add_up(value):
-        return jnp.broadcast_to(jnp.sum(value, keepdims=True), (SUB, LANE))
+        for shift in (4, 2, 1):
+            value = value + pltpu.roll(value, shift, 0)
+        return jnp.broadcast_to(jnp.sum(value, axis=1, keepdims=True), (SUB, LANE))
 
     pairs = [(j, i) for j in range(size) for i in range(j, size)]
 
@@ -259,6 +287,22 @@
     def half_type(value):
         return value.astype(jnp.bfloat16).astype(jnp.float32)
 
+    def out_copy(g, owner):
+        return pltpu.make_async_remote_copy(
+            src_ref=dos.at[g], dst_ref=out_recv.at[owner], send_sem=out_send.at[g],
+            recv_sem=out_recv_sem.at[owner], device_id=(g, h_me), device_id_type=MESH)
+
+    owner = g_me < targets
+
+    def finish(*finished):
+        for g in finished:
+            at = pl.ds(g * slots, local_m)
+            top = jnp.sum(jnp.sum(numer[at], axis=1), axis=1, keepdims=True)
+            low = jnp.sum(jnp.sum(denom[at], axis=1), axis=1, keepdims=True)
+            dos[g, 0:local_m, :] = jnp.broadcast_to(top / low, (local_m, LANE))
+        for g in finished:
+            pl.when((g != g_me) & owner)(out_copy(g, g_me).start)
+
     def score_section(s, carry):
         def step(n, carry):
             f, b = list(carry[:vecs]), list(carry[vecs:])
@@ -289,28 +333,18 @@
                 numer[b_order[i]], denom[b_order[i]] = tops[1, i], lows[1, i]
             return tuple(f) + tuple(b)
 
-        return lax.fori_loop(0, blocks, step, carry)
+        carry = lax.fori_loop(0, blocks, step, carry)
+        finish(s, groups - 1 - s)
+        return carry
 
     carry = lax.fori_loop(0, half, store_section, tuple(fwd) + tuple(bwd))
     lax.fori_loop(half, groups, score_section, carry)
 
-    def out_copy(g, owner):
-        return pltpu.make_async_remote_copy(
-            src_ref=dos.at[g], dst_ref=out_recv.at[owner], send_sem=out_send.at[g],
-            recv_sem=out_recv_sem.at[owner], device_id=(g, h_me), device_id_type=MESH)
-
-    owner = g_me < targets
-
-    @pl.loop(0, groups, unroll=min(groups, 4))
-    def _(g):
-        at = pl.ds(g * slots, local_m)
-        top = jnp.sum(jnp.sum(numer[at], axis=1), axis=1, keepdims=True)
-        low = jnp.sum(jnp.sum(denom[at], axis=1), axis=1, keepdims=True)
-        dos[g, 0:local_m, :] = jnp.broadcast_to(top / low, (local_m, LANE))
-
-        @pl.when((g != g_me) & owner)
-        def _():
-            out_copy(g, g_me).start()
+    @pl.loop(1, groups)
+    def _(d):
+        meta_copy(lax.rem(g_me + d, groups), g_me).wait_send()
+
+    each_peer(lambda g, h: block_copy(g, h, g_me, h_me).wait_send())
 
     @pl.when(owner)
     def _():
@@ -328,19 +362,11 @@
         result = jnp.where(lane_m == t, out_recv[t, 0:local_m, :], result)
     out[...] = result[:, 0:targets]
 
-    @pl.loop(1, groups)
-    def _(d):
-        g = lax.rem(g_me + d, groups)
-        meta_copy(g, g_me).wait_send()
-
-        @pl.when(owner)
-        def _():
-            out_copy(g, g_me).wait_send()
-
-    @pl.loop(1, devices)
-    def _(d):
-        peer = lax.rem(me + d, devices)
-        block_copy(peer // haps, lax.rem(peer, haps), g_me, h_me).wait_send()
+    @pl.when(owner)
+    def _():
+        @pl.loop(1, groups)
+        def _(d):
+            out_copy(lax.rem(g_me + d, groups), g_me).wait_send()
 
 
 def solution(mesh):
@@ -357,7 +383,7 @@
         slots = pack * -(-local_m // pack)
         markers = local_m * groups
         size = block_size(local_m)
-        assert targets <= groups and groups % 2 == 0 and slots % SUB == 0
+        assert targets < SUB and targets <= groups and groups % 2 == 0 and slots % SUB == 0
         vmem = pl.BlockSpec(memory_space=pltpu.VMEM)
         dims = (groups, haps, local_m, targets, words, bits_word)
         f32, i32 = jnp.float32, jnp.int32
@@ -365,14 +391,14 @@
         return pl.pallas_call(
             functools.partial(kernel, dims),
             out_shape=jax.ShapeDtypeStruct((local_m, targets), f32),
-            in_specs=[vmem, vmem, pl.BlockSpec(memory_space=pltpu.SMEM), vmem, vmem],
+            in_specs=[vmem, vmem, pl.BlockSpec(memory_space=pltpu.SMEM)] + [pl.BlockSpec(memory_space=pltpu.HBM)] * 2,
             out_specs=vmem,
             scratch_shapes=[
                 pltpu.VMEM((slots + SUB, LANE), i32),
-                pltpu.VMEM((slots, LANE), i32),
+                pltpu.VMEM((SUB, LANE), i32),
                 pltpu.VMEM((SUB, LANE), i32),
                 pltpu.VMEM((groups, haps * SUB, LANE), i32),
-                pltpu.VMEM((groups, slots, LANE), i32),
+                pltpu.VMEM((groups, SUB, LANE), i32),
                 pltpu.VMEM((groups * slots, SUB, LANE), i32),
                 pltpu.VMEM((4, groups * slots, LANE), f32),
                 pltpu.VMEM((vecs * SUB * targets, LANE), f32),
@@ -384,12 +410,13 @@
                 pltpu.VMEM((groups * slots, SUB, LANE), f32),
                 pltpu.VMEM((groups, slots, LANE), f32),
                 pltpu.VMEM((targets, slots, LANE), f32),
+                pltpu.VMEM((targets, total_haps), f32), pltpu.VMEM((targets, total_haps), f32), dma((2,)),
                 dma((groups, haps)), dma((groups, haps)),
                 dma((groups,)), dma((groups,)), dma((groups,)), dma((targets,)),
             ],
             compiler_params=pltpu.CompilerParams(
-                collective_id=0, has_side_effects=True, vmem_limit_bytes=48 * 1024 * 1024),
-        )(alleles, observed, map_steps, start_weights, end_weights)
+                collective_id=0, has_side_effects=True, vmem_limit_bytes=60 * 1024 * 1024),
+        )(alleles, observed.T, map_steps, start_weights, end_weights)
 
     in_specs = (P("grp", "hap"), P("grp", "hap"), P("grp"), P("hap", None), P("hap", None))
     return jax.shard_map(local, mesh=mesh, in_specs=in_specs, out_specs=P("grp", "hap"), check_vma=False)

time: 27 us -> 24 us (0.89)
  local copies, waits for them, and re-layouts: 3.35 us -> 1.35 us
  Pallas kernels: 23.4 us -> 22.3 us
    unnamed x9 -> x0, local copies, waits for them, and re-layouts: 2.69 us -> none
    pallas_call x1, Pallas kernels: 23.4 us -> 22.3 us  [local(): pl.pallas_call(functools.partial(kernel, dims), out_shape=jax.ShapeDtypeS...]
    pallas_call x1, local copies, waits for them, and re-layouts: 0.66 us -> 1.35 us  [local(): pl.pallas_call(functools.partial(kernel, dims), out_shape=jax.ShapeDtypeS...]
where the time goes in v3:
time: 24 us; the launch traced here: 23.7 us
  Pallas kernels  22.3 us (93%)
  local copies, waits for them, and re-layouts  1.35 us (6%)
    pallas_call x1, Pallas kernels, local(): pl.pallas_call(functools.partial(kernel, dims), out_shape=jax.ShapeDtypeS...  22.3 us
    pallas_call x1, local copies, waits for them, and re-layouts, local(): pl.pallas_call(functools.partial(kernel, dims), out_shape=jax.ShapeDtypeS...  1.35 us

profile of v3, /device:TPU:0, one launch (start us, length us, event | category | flops | bytes accessed | tf_op | source)
XLA Modules:
  0.0 23.7 jit_solution(3440674338377870949)
XLA Ops:
  0.0 22.3 %shard_map.55 = f32[15,4]{1,0:T(8,128)} custom-call(s32[15,64]{1,0:T(8,128)} %alleles.1, s32[4,15]{1,0:T(4,128)} %bitcast.1, s32[15]{0:T(128)} %steps.1, f32[4,15360]{1,0:T(4,128)} %starts.1, f32[4,15360]{1,0:T(4,128)} %ends.1), custom_call_target="tpu_custom_call" | custom-call | tf_op jit(solution)/shard_map/pallas_call | solution.py:391
  22.4 1.4 %copy.6 = f32[15,4]{0,1:T(4,128)} copy(f32[15,4]{1,0:T(8,128)} %shard_map.55) | data formatting | bytes 480 | tf_op jit(solution)/shard_map/pallas_call | solution.py:391
